TPU v7x, 512 devices: a whole 4x8x8 slice. The times are simulated.
512 devices in a mesh: chan: 16 (over x, y_lo), slab: 32 (over z, y_hi, core).
Axes of the slice: x: 4, y: 8 (y_hi: 2, y_lo: 4; y = y_hi * 4 + y_lo), z: 8, core: 2. Of those that a mesh axis runs over, the one named last changes fastest.
Arguments:
- taylor_models: float32 [2, 2048, 2048], P(None, 'slab', 'chan'), may hold values from -6 to 6
- gridded_vis: bfloat16 [16, 2, 2048, 2048], P('chan', None, 'slab'), may hold values from -6 to 6
- uv_weight: bfloat16 [16, 2048, 2048], P('chan', 'slab'), may hold values from 0 to 2
- freq_ratio: float32 [16], P('chan'), may hold values from 0.6 to 1.4
- robust_scale: float32 [16], P('chan'), may hold values from 0.25 to 4
Outputs:
- taylor_residual: float32 [2, 2048, 2048], P(None, 'slab', 'chan')
All inputs are finite; a program needn't handle non-finite values.
Results may differ from a plain program's by a relative error of at most 0.0003.
Values sent between devices are 32-bit elements; how exact they have to be, the bound alone decides.
A program may use at most 64 MiB of HBM per device.

v0:
```python
import functools

import jax
import jax.numpy as jnp
import numpy as np
from jax import lax
from jax.experimental import pallas as pl
from jax.experimental.pallas import tpu as pltpu
from jax.sharding import PartitionSpec as P

PIX = 2048
F32, BF16 = jnp.float32, jnp.bfloat16
MESH = pl.DeviceIdType.MESH
NC, NS, NX = 16, 32, 4


def rep(angle):
    c, s = np.cos(angle), np.sin(angle)
    return np.array([[c, s], [-s, c]])


def tables():
    tau = 2 * np.pi
    j, c = np.arange(16), np.arange(16)
    ang = tau * np.outer(j, c) / 16
    first = np.stack([np.cos(ang), -np.sin(ang)])
    t_a = np.einsum("ijc,rq->ijrcq", first, np.eye(8)).reshape(256, 128)
    ang = np.repeat(tau * np.outer(j, np.arange(128)) / PIX, 8, axis=0)
    w_a = np.stack([np.cos(ang), -np.sin(ang)])
    b = rep(tau * np.outer(np.arange(128), np.arange(128)) / 128)
    t_b = np.einsum("oika->koia", b).reshape(256, 256)
    y1 = 8 * np.arange(32)[None, :] + np.arange(8)[:, None]
    d = rep(tau * (np.arange(256)[:, None, None] * y1 % 256) / 256)
    t_d = np.einsum("oipgs->opgis", d).reshape(512, 512)
    ang = np.tile(tau * np.outer(np.arange(256), np.arange(8)) / PIX, (1, 16))
    w_d = np.stack([np.cos(ang), -np.sin(ang)]) / PIX
    e = rep(tau * np.outer(np.arange(8), np.arange(8)) / 8)
    t_e = np.einsum("oimr,jq->omjiqr", e, np.eye(16)).reshape(256, 256)
    return [x.astype(np.float32) for x in (t_a, w_a, t_b, t_d, w_d, t_e)]


def split(x):
    hi = x.astype(BF16)
    return hi, (x - hi.astype(F32)).astype(BF16)


def dot3(a, b, nt):
    dims = (((1,), (1 if nt else 0,)), ((), ()))

    def one(p, q):
        return lax.dot_general(p, q, dims, preferred_element_type=F32)

    return one(a[0], b[0]) + one(a[0], b[1]) + one(a[1], b[0])


def both(ref):
    return ref[0], ref[1]


def kernel(
    freq, robust, taylor, vis, wt, t_a, w_a, t_b, t_d, w_d, t_e, out,
    tay_v, vis_v, wt_v, va, vwa, vb, vd, vwd, ve,
    ma, mat, mb, md, mdt, me2, met, vwdt,
    buf1, snd2, buf2, snd3, buf3, fs, ws, snd5, buf5, snd6, buf6, snd7, buf7,
    vsend, vrecv, prm,
    lsem, s1, s2, s3, s5, s6, s7, sv, sp, r1, r2, r3, r5, r6, r7, rv, rp,
):
    chan, slab = lax.axis_index("chan"), lax.axis_index("slab")
    mx, my = chan // 4, chan % 4

    loads = [
        pltpu.make_async_copy(src, dst, lsem.at[i])
        for i, (src, dst) in enumerate(
            [(taylor, tay_v), (vis, vis_v), (wt, wt_v), (t_a, va), (w_a, vwa),
             (t_b, vb), (t_d, vd), (w_d, vwd), (t_e, ve)]
        )
    ]
    for cp in loads:
        cp.start()

    barrier = pltpu.get_barrier_semaphore()

    def greet_slab(d, _):
        pl.semaphore_signal(barrier, inc=1, device_id={"slab": (slab + d) % NS}, device_id_type=MESH)
        return 0

    def greet_chan(d, _):
        pl.semaphore_signal(barrier, inc=1, device_id={"chan": (chan + d) % NC}, device_id_type=MESH)
        return 0

    lax.fori_loop(1, NS, greet_slab, 0)
    lax.fori_loop(1, NC, greet_chan, 0)

    rows = lax.broadcasted_iota(jnp.int32, (8, 128), 0)
    prm[pl.ds(mx, 1)] = jnp.where(rows == 0, freq[0] - 1.0, robust[0])[None]
    loads[1].wait()
    loads[2].wait()
    for q in range(NX):
        for p in range(2):
            vsend[q, p] = vis_v[p, 16 * q : 16 * q + 16].astype(F32)
        vsend[q, 2] = wt_v[16 * q : 16 * q + 16].astype(F32)
    loads[0].wait()

    pl.semaphore_wait(barrier, NS + NC - 2)

    def tile(ref, i, n=8):
        return ref.at[pl.ds(pl.multiple_of(i * n, n), n)]

    def to_chan(src, dst, n, send, recv, d):
        peer = (chan + d) % NC
        return pltpu.make_async_remote_copy(
            tile(src, peer, n), tile(dst, chan, n), send.at[d], recv,
            device_id={"chan": peer}, device_id_type=MESH)

    def to_slab(src, dst, send, recv, d):
        peer = (slab + d) % NS
        return pltpu.make_async_remote_copy(
            tile(src, peer), tile(dst, slab), send.at[d], recv,
            device_id={"slab": peer}, device_id_type=MESH)

    def go(make, n):
        def step(d, _):
            make(d).start()
            return 0
        lax.fori_loop(1, n, step, 0)

    def sent(make, n):
        def step(d, _):
            make(d).wait_send()
            return 0
        lax.fori_loop(1, n, step, 0)

    def landed(buf, sem):
        pltpu.make_async_copy(buf, buf, sem).wait()

    x1 = functools.partial(to_chan, tay_v, buf1, 8, s1, r1)
    go(x1, NC)
    pltpu.make_async_copy(tile(tay_v, chan), tile(buf1, chan), r1).start()

    def xp(d):
        return pltpu.make_async_remote_copy(
            prm.at[mx], prm.at[mx], sp.at[d], rp.at[d],
            device_id={"chan": (mx + d) % NX * 4 + my}, device_id_type=MESH)

    def xv(d):
        peer = (mx + d) % NX
        return pltpu.make_async_remote_copy(
            vsend.at[peer], vrecv.at[d - 1], sv.at[d], rv.at[d],
            device_id={"chan": peer * 4 + my}, device_id_type=MESH)

    for d in (1, 3, 2):
        xp(d).start()
    for d in (1, 3, 2):
        xv(d).start()

    def put(dst, x):
        dst[0], dst[1] = split(x)

    for i in (3, 4, 5):
        loads[i].wait()
    put(ma, va[...])
    put(mb, vb[...])

    landed(buf1, r1)
    pre = dot3(both(ma), split(buf1[...]), False)
    re, im = pre[:128], pre[128:]
    yre = re * vwa[0] - im * vwa[1]
    yim = re * vwa[1] + im * vwa[0]
    snd2[...] = dot3(both(mb), split(jnp.concatenate([yre, yim], axis=1)), True)

    x2 = functools.partial(to_slab, snd2, buf2, s2, r2)
    go(x2, NS)
    pltpu.make_async_copy(tile(snd2, slab), tile(buf2, slab), r2).start()

    for i in (6, 7, 8):
        loads[i].wait()
    put(md, vd[...])
    put(me2, ve[...])
    put(mat, va[...].T)
    put(met, ve[...].T)
    put(mdt, vd[...].T)
    vwdt[0] = vwd[0].T
    vwdt[1] = vwd[1].T

    landed(buf2, r2)
    for q in range(4):
        for p in range(2):
            snd3[pl.ds(64 * q + 32 * p, 32)] = buf2[pl.ds(2 * q + p, 32, stride=8)]

    def x3(d):
        peer = (chan + d) % NC
        return pltpu.make_async_remote_copy(
            tile(snd3, peer // 4, 64), tile(buf3, chan, 64), s3.at[d], r3,
            device_id={"chan": peer}, device_id_type=MESH)

    go(x3, NC)
    pltpu.make_async_copy(tile(snd3, mx, 64), tile(buf3, chan, 64), r3).start()
    landed(buf3, r3)

    x = jnp.concatenate([buf3[:512], buf3[512:]], axis=1)
    pre = dot3(both(md), split(x), False)
    parts = []
    for t in range(2):
        re, im = pre[:256, 128 * t : 128 * t + 128], pre[256:, 128 * t : 128 * t + 128]
        parts.append(jnp.concatenate(
            [re * vwd[0] - im * vwd[1], re * vwd[1] + im * vwd[0]], axis=1))
    fs[...] = dot3(both(me2), split(jnp.concatenate(parts, axis=0)), True)

    for d in (1, 3, 2):
        xp(d).wait_recv()
        xv(d).wait_recv()

    def point(m, _):
        lo, hi = pl.ds(pl.multiple_of(16 * m, 16), 16), pl.ds(pl.multiple_of(128 + 16 * m, 16), 16)
        lane = pl.ds(pl.multiple_of(256 * m, 256), 256)
        f0r, f1r = fs[lo, :256], fs[lo, 256:]
        f0i, f1i = fs[hi, :256], fs[hi, 256:]
        sums = [jnp.zeros((16, 256), F32)] * 4
        for d in range(NX):
            who = (mx - d + NX) % NX
            pair = prm[pl.ds(who, 1)][0]
            off, damp = pair[0:1, 0:1], pair[1:2, 0:1]
            if d == 0:
                vr, vi, w = (vsend[pl.ds(mx, 1), p, :, lane][0] for p in range(3))
            else:
                vr, vi, w = (vrecv[d - 1, p, :, lane] for p in range(3))
            dr = vr - w * (f0r + off * f1r)
            di = vi - w * (f0i + off * f1i)
            k = 1.0 / (1.0 + damp * (dr * dr + di * di))
            wr, wi = k * dr, k * di
            sums = [sums[0] + wr, sums[1] + wi, sums[2] + off * wr, sums[3] + off * wi]
        ws[lo, :256], ws[hi, :256], ws[lo, 256:], ws[hi, 256:] = sums
        return 0

    lax.fori_loop(0, 8, point, 0)

    pre = dot3(both(met), split(ws[...]), False)
    parts = []
    for t in range(2):
        re, im = pre[:128, 256 * t : 256 * t + 256], pre[128:, 256 * t : 256 * t + 256]
        parts.append(jnp.concatenate(
            [re * vwdt[0] + im * vwdt[1], im * vwdt[0] - re * vwdt[1]], axis=1))
    back = dot3(both(mdt), split(jnp.concatenate(parts, axis=0)), True)
    snd5[:512] = back[:, :128]
    snd5[512:] = back[:, 128:]

    x5 = functools.partial(to_chan, snd5, buf5, 64, s5, r5)
    go(x5, NC)
    pltpu.make_async_copy(tile(snd5, chan, 64), tile(buf5, chan, 64), r5).start()
    landed(buf5, r5)
    for q in range(4):
        b = 256 * q
        acc = (buf5[b : b + 64] + buf5[b + 64 : b + 128]) + (buf5[b + 128 : b + 192] + buf5[b + 192 : b + 256])
        for p in range(2):
            snd6[pl.ds(2 * q + p, 32, stride=8)] = acc[32 * p : 32 * p + 32]

    x6 = functools.partial(to_slab, snd6, buf6, s6, r6)
    go(x6, NS)
    pltpu.make_async_copy(tile(snd6, slab), tile(buf6, slab), r6).start()
    landed(buf6, r6)
    z = dot3(split(buf6[...].T), both(mb), False)
    re, im = z[:, :128], z[:, 128:]
    z = jnp.concatenate([re * vwa[0] + im * vwa[1], im * vwa[0] - re * vwa[1]], axis=0)
    snd7[...] = dot3(both(mat), split(z), False)

    x7 = functools.partial(to_chan, snd7, buf7, 8, s7, r7)
    go(x7, NC)
    pltpu.make_async_copy(tile(snd7, chan), tile(buf7, chan), r7).start()

    sent(x1, NC)
    sent(x2, NS)
    sent(x3, NC)
    sent(x5, NC)
    sent(x6, NS)
    for d in (1, 3, 2):
        xp(d).wait_send()
        xv(d).wait_send()
    sent(x7, NC)
    landed(buf7, r7)
    out[...] = buf7[...]


def local(taylor_models, gridded_vis, uv_weight, freq_ratio, robust_scale):
    tabs = [jnp.asarray(x) for x in tables()]
    any_space = pl.BlockSpec(memory_space=pl.ANY)
    smem = pl.BlockSpec(memory_space=pltpu.SMEM)
    v = pltpu.VMEM
    dma = pltpu.SemaphoreType.DMA
    scratch = (
        [v((128, 128), F32), v((2, 64, PIX), BF16), v((64, PIX), BF16)]
        + [v(x.shape, F32) for x in tabs]
        + [v((2, *s), BF16) for s in
           ((256, 128), (128, 256), (256, 256), (512, 512), (512, 512), (256, 256), (256, 256))]
        + [v((2, 128, 256), F32)]
        + [v((n, m), F32) for n, m in
           ((128, 128), (256, 128), (256, 128), (256, 128), (1024, 128), (256, 512), (256, 512),
            (1024, 128), (1024, 128), (256, 128), (256, 128), (128, 128), (128, 128))]
        + [v((4, 3, 16, PIX), F32), v((3, 3, 16, PIX), F32), v((4, 8, 128), F32)]
        + [dma((9,)), dma((NC,)), dma((NS,)), dma((NC,)), dma((NC,)), dma((NS,)), dma((NC,)),
           dma((4,)), dma((4,))]
        + [dma, dma, dma, dma, dma, dma, dma((4,)), dma((4,))]
    )
    out = pl.pallas_call(
        kernel,
        out_shape=jax.ShapeDtypeStruct((128, 128), F32),
        in_specs=[smem, smem] + [any_space] * 9,
        out_specs=pl.BlockSpec(memory_space=pltpu.VMEM),
        scratch_shapes=scratch,
        compiler_params=pltpu.CompilerParams(
            collective_id=0, has_side_effects=True, vmem_limit_bytes=40 * 1024 * 1024),
    )(freq_ratio, robust_scale, taylor_models.reshape(128, 128), gridded_vis[0], uv_weight[0], *tabs)
    return out.reshape(2, 64, 128)


def solution(mesh):
    placed = (
        P(None, "slab", "chan"),
        P("chan", None, "slab", None),
        P("chan", "slab", None),
        P("chan"),
        P("chan"),
    )
    return jax.shard_map(
        local, mesh=mesh, in_specs=placed, out_specs=P(None, "slab", "chan"), check_vma=False
    )
```

profile of v0, /device:TPU:1, one launch (start us, length us, event | category | flops | bytes accessed | tf_op | source)
XLA Modules:
  0.0 86.5 jit_solution(12974535038250689127)
XLA Ops:
  1.3 0.0 copy-start
  1.3 1.2 %copy-done = f32[512,512]{1,0:T(8,128)S(1)} copy-done((f32[512,512]{1,0:T(8,128)S(1)}, f32[512,512]{1,0:T(8,128)}, u32[]{:S(2)}) %copy-start) | copy-done | bytes 1048600
  2.5 0.0 copy-start.1
  2.5 1.0 %copy-done.1 = bf16[1,2,64,2048]{3,2,1,0:T(8,128)(2,1)S(1)} copy-done((bf16[1,2,64,2048]{3,2,1,0:T(8,128)(2,1)S(1)}, bf16[1,2,64,2048]{3,2,1,0:T(8,128)(2,1)}, u32[]{:S(2)}) %copy-start.1) | copy-done | bytes 524312
  3.6 0.0 copy-start.2
  3.6 0.9 %copy-done.2 = bf16[1,64,2048]{2,1,0:T(8,128)(2,1)S(1)} copy-done((bf16[1,64,2048]{2,1,0:T(8,128)(2,1)S(1)}, bf16[1,64,2048]{2,1,0:T(8,128)(2,1)}, u32[]{:S(2)}) %copy-start.2) | copy-done | bytes 262168
  4.5 0.0 copy-start.3
  4.5 0.9 %copy-done.3 = f32[256,256]{1,0:T(8,128)S(1)} copy-done((f32[256,256]{1,0:T(8,128)S(1)}, f32[256,256]{1,0:T(8,128)}, u32[]{:S(2)}) %copy-start.3) | copy-done | bytes 262168
  5.5 0.0 copy-start.4
  5.5 0.9 %copy-done.4 = f32[2,256,128]{2,1,0:T(8,128)S(1)} copy-done((f32[2,256,128]{2,1,0:T(8,128)S(1)}, f32[2,256,128]{2,1,0:T(8,128)}, u32[]{:S(2)}) %copy-start.4) | copy-done | bytes 262168
  6.4 0.0 copy-start.5
  6.4 0.9 %copy-done.5 = f32[256,256]{1,0:T(8,128)S(1)} copy-done((f32[256,256]{1,0:T(8,128)S(1)}, f32[256,256]{1,0:T(8,128)}, u32[]{:S(2)}) %copy-start.5) | copy-done | bytes 262168
  7.4 0.0 copy-start.6
  7.4 0.9 %copy-done.6 = f32[2,128,128]{2,1,0:T(8,128)S(1)} copy-done((f32[2,128,128]{2,1,0:T(8,128)S(1)}, f32[2,128,128]{2,1,0:T(8,128)}, u32[]{:S(2)}) %copy-start.6) | copy-done | bytes 131096
  8.3 0.0 copy-start.7
  8.3 0.9 %copy-done.7 = f32[256,128]{1,0:T(8,128)S(1)} copy-done((f32[256,128]{1,0:T(8,128)S(1)}, f32[256,128]{1,0:T(8,128)}, u32[]{:S(2)}) %copy-start.7) | copy-done | bytes 131096
  9.2 0.0 copy-start.8
  9.2 0.8 copy-done.8
  10.0 75.8 %shard_map.109 = f32[128,128]{1,0:T(8,128)S(1)} custom-call(f32[1]{0:T(128)S(6)} %copy.13.freq, f32[1]{0:T(128)S(6)} %copy.14.robust, f32[128,128]{1,0:T(8,128)S(1)} %bitcast.7, bf16[2,64,2048]{2,1,0:T(8,128)(2,1)S(1)} %bitcast.4, bf16[64,2048]{1,0:T(8,128)(2,1)S(1)} %bitcast.6, f32[256,128]{1,0:T(8,128)S(1)} %copy-done.7, f32[2,128,128]{2,1,0:T(8,128)S(1)} %copy-done.6, ...), custom_call_target="tpu_custom_call" | custom-call | tf_op jit(solution)/shard_map/pallas_call | solution.py:303
  85.8 0.6 copy.15
Async XLA Ops:
  1.3 1.2 %copy-start = (f32[512,512]{1,0:T(8,128)S(1)}, f32[512,512]{1,0:T(8,128)}, u32[]{:S(2)}) copy-start(f32[512,512]{1,0:T(8,128)} %constant.15.clone.t_d) | copy-start | bytes 3145732
  2.5 1.0 %copy-start.1 = (bf16[1,2,64,2048]{3,2,1,0:T(8,128)(2,1)S(1)}, bf16[1,2,64,2048]{3,2,1,0:T(8,128)(2,1)}, u32[]{:S(2)}) copy-start(bf16[1,2,64,2048]{3,2,1,0:T(8,128)(2,1)} %param.12) | copy-start | bytes 1572868
  3.6 0.9 %copy-start.2 = (bf16[1,64,2048]{2,1,0:T(8,128)(2,1)S(1)}, bf16[1,64,2048]{2,1,0:T(8,128)(2,1)}, u32[]{:S(2)}) copy-start(bf16[1,64,2048]{2,1,0:T(8,128)(2,1)} %param.13) | copy-start | bytes 786436
  4.5 0.9 %copy-start.3 = (f32[256,256]{1,0:T(8,128)S(1)}, f32[256,256]{1,0:T(8,128)}, u32[]{:S(2)}) copy-start(f32[256,256]{1,0:T(8,128)} %constant.17.clone.t_e) | copy-start | bytes 786436
  5.5 0.9 %copy-start.4 = (f32[2,256,128]{2,1,0:T(8,128)S(1)}, f32[2,256,128]{2,1,0:T(8,128)}, u32[]{:S(2)}) copy-start(f32[2,256,128]{2,1,0:T(8,128)} %constant.16.clone.w_d) | copy-start | bytes 786436
  6.4 0.9 %copy-start.5 = (f32[256,256]{1,0:T(8,128)S(1)}, f32[256,256]{1,0:T(8,128)}, u32[]{:S(2)}) copy-start(f32[256,256]{1,0:T(8,128)} %constant.14.clone.t_b) | copy-start | bytes 786436
  7.4 0.9 %copy-start.6 = (f32[2,128,128]{2,1,0:T(8,128)S(1)}, f32[2,128,128]{2,1,0:T(8,128)}, u32[]{:S(2)}) copy-start(f32[2,128,128]{2,1,0:T(8,128)} %constant.13.clone.w_a) | copy-start | bytes 393220
  8.3 0.9 %copy-start.7 = (f32[256,128]{1,0:T(8,128)S(1)}, f32[256,128]{1,0:T(8,128)}, u32[]{:S(2)}) copy-start(f32[256,128]{1,0:T(8,128)} %constant.12.clone.t_a) | copy-start | bytes 393220
  9.2 0.8 copy-start.8
where the time goes:
time: 86.9 us; the launch traced here: 86.5 us
  Pallas kernels  75.8 us (87%)
  local copies, waits for them, and re-layouts  9.34 us (11%)
  between operations  1.32 us (2%)
    pallas_call x1, Pallas kernels, local(): pl.pallas_call(kernel, out_shape=jax.ShapeDtypeStruct((128, 128), F32), i...  75.8 us
    unnamed x19, local copies, waits for them, and re-layouts  9.34 us

commit v1 on v0

v1 whole, which is shorter than its diff:
```python
import functools

import jax
import jax.numpy as jnp
import numpy as np
from jax import lax
from jax.experimental import pallas as pl
from jax.experimental.pallas import tpu as pltpu
from jax.sharding import PartitionSpec as P

PIX = 2048
F32, BF16 = jnp.float32, jnp.bfloat16
MESH = pl.DeviceIdType.MESH
NC, NZ, NY = 16, 16, 32


EARLY, LATE = (2, 6, 1, 3, 7), (4, 5)


def rep(angle):
    c, s = np.cos(angle), np.sin(angle)
    return np.array([[c, s], [-s, c]])


def tables():
    tau = 2 * np.pi
    j, c = np.arange(16), np.arange(16)
    ang = tau * np.outer(j, c) / 16
    first = np.stack([np.cos(ang), -np.sin(ang)])
    t_a = np.einsum("ijc,rq->ijrcq", first, np.eye(8)).reshape(256, 128)
    ang = np.repeat(tau * np.outer(j, np.arange(128)) / PIX, 8, axis=0)
    w_a = np.stack([np.cos(ang), -np.sin(ang)])
    z, k, h, q = np.meshgrid(*map(np.arange, (8, 2, 2, 4)), indexing="ij")
    step = (((z * 2 + h) * 2 + k) * 4 + q).reshape(128)
    t_b = np.einsum("oika->okia", rep(tau * np.outer(step, np.arange(128)) / 128)).reshape(256, 256)
    h, g, z, k = np.meshgrid(*map(np.arange, (2, 8, 8, 2)), indexing="ij")
    y1 = (8 * ((z * 2 + h) * 2 + k) + g).reshape(256)
    ang = tau * (np.outer(np.arange(256), y1) % 256) / 256
    t_d = np.concatenate([np.cos(ang), np.sin(ang)])
    ang = np.tile(tau * np.outer(np.arange(256), np.arange(8)) / PIX, (1, 8))
    w_d = np.stack([np.tile(np.cos(ang), (1, 2)), np.concatenate([np.sin(ang), -np.sin(ang)], axis=1)]) / PIX
    e = rep(tau * np.outer(np.arange(8), np.arange(8)) / 8)
    t_e = np.einsum("oimr,jq->omjiqr", e, np.eye(8)).reshape(128, 128)
    return [x.astype(np.float32) for x in (t_a, w_a, t_b, t_d, w_d, t_e)]


def split(x):
    hi = x.astype(BF16)
    return hi, (x - hi.astype(F32)).astype(BF16)


def dot3(a, b, nt):
    dims = (((1,), (1 if nt else 0,)), ((), ()))

    def one(p, q):
        return lax.dot_general(p, q, dims, preferred_element_type=F32)

    return one(a[0], b[0]) + one(a[0], b[1]) + one(a[1], b[0])


def both(ref):
    return ref[0], ref[1]


def swap(x):
    return pltpu.roll(x, 64, axis=1)


def kernel(
    freq, robust, taylor, vis, wt, t_a, w_a, t_b, t_d, w_d, t_e, out,
    freq_s, robust_s, tay_v, vis_v, wt_v, va, vwa, vb, vd, vwd, ve,
    ma, mat, mb, md, mdt, me2, met, vwdt,
    buf1, snd2, buf2, snd3, buf3, fs, ws, snd5, buf5, snd6, buf6, snd7, buf7,
    vsend, vrecv, prm,
    lsem, s1, s2, s3, s5, s6, s7, sv, sp, r1, r2, r3, r5, r6, r7, rv, rp,
):
    def turn(i, d, n):
        return lax.rem(i + d, n)

    chan, slab = lax.axis_index("chan"), lax.axis_index("slab")
    mx, my = lax.div(chan, 4), lax.rem(chan, 4)
    mp, me = lax.div(my, 2), lax.rem(my, 2)
    mk, mh, z = lax.rem(slab, 2), lax.rem(lax.div(slab, 2), 2), lax.div(slab, 4)
    mz = z * 2 + mk
    mo = mx * 2 + me
    xs, ys = [turn(mx, d, 4) for d in range(4)], [turn(my, d, 4) for d in range(4)]
    hs, ks = [mh, 1 - mh], [mk, 1 - mk]
    es = [lax.rem(y, 2) for y in ys]
    x_rows = [lax.div(x, 2) * 16 + lax.rem(x, 2) * 4 for x in xs]
    slab_h = [slab, slab + 2 - 4 * mh]
    FAR = (2, 3, 1, 0)

    chan_peers = [
        (xs[i] * 4 + ys[j], {"chan": xs[i] * 4 + ys[j]}) for i in FAR for j in FAR if i or j]
    y_peers = [
        (hs[h] * 8 + xs[i] * 2 + es[j], x_rows[i] + hs[h] * 8 + ys[j],
         {"chan": xs[i] * 4 + ys[j], "slab": slab_h[h]})
        for h in (1, 0) for i in FAR for j in FAR if h or i or j]
    z_peers = []
    for d in (4, 3, 5, 2, 6, 1, 7, 0):
        for k in (1, 0):
            if d or k:
                far = turn(z, d, 8)
                z_peers.append((far * 2 + ks[k], {"slab": far * 4 + mh * 2 + ks[k]}))
    my_row, my_u = x_rows[0] + mh * 8 + my, mh * 8 + mo

    barrier = pltpu.get_barrier_semaphore()
    for peer in y_peers + z_peers:
        pl.semaphore_signal(barrier, inc=1, device_id=peer[-1], device_id_type=MESH)

    loads = [
        pltpu.make_async_copy(src, dst, lsem.at[i])
        for i, (src, dst) in enumerate(
            [(taylor, tay_v), (vis, vis_v), (wt, wt_v), (t_a, va), (w_a, vwa),
             (t_b, vb), (t_d, vd), (w_d, vwd), (t_e, ve), (freq, freq_s), (robust, robust_s)]
        )
    ]
    for i in (9, 10, 0, 1, 2, 3, 4, 5, 6, 7, 8):
        loads[i].start()

    rows = lax.broadcasted_iota(jnp.int32, (8, 128), 0)
    loads[9].wait()
    loads[10].wait()
    prm[pl.ds(mo, 1)] = jnp.where(rows == 0, freq_s[0] - 1.0, robust_s[0])[None]
    loads[1].wait()
    loads[2].wait()
    for q in range(4):
        for p in range(3):
            src = wt_v[16 * q : 16 * q + 16] if p == 2 else vis_v[p, 16 * q : 16 * q + 16]
            wide = src.astype(F32)
            vsend[2 * q, p] = wide[:8]
            vsend[2 * q + 1, p] = wide[8:]
    loads[0].wait()

    pl.semaphore_wait(barrier, len(y_peers) + len(z_peers))

    def tile(ref, i, n=8):
        return ref.at[pl.ds(pl.multiple_of(i * n, n), n)]

    def spread(peers, src, dst, mine, kept, n, send, recv, which=0):
        for peer in peers:
            pltpu.make_async_remote_copy(
                tile(src, peer[which], n), tile(dst, mine, n), send, recv,
                device_id=peer[-1], device_id_type=MESH).start()
        pltpu.make_async_copy(tile(src, kept, n), tile(dst, mine, n), recv).start()

    def landed(buf, sem):
        pltpu.make_async_copy(buf, buf, sem).wait()

    spread(chan_peers, tay_v, buf1, chan, chan, 8, s1, r1)

    def ally(d):
        x, e = xs[d // 2], es[d % 2]
        return x * 2 + e, {"chan": x * 4 + mp * 2 + e}

    def xp(d):
        return pltpu.make_async_remote_copy(
            prm.at[mo], prm.at[mo], sp, rp.at[d], device_id=ally(d)[1], device_id_type=MESH)

    def xv(d):
        o, device = ally(d)
        return pltpu.make_async_remote_copy(
            vsend.at[o], vrecv.at[d - 1], sv, rv.at[d], device_id=device, device_id_type=MESH)

    for d in EARLY + LATE:
        xp(d).start()
    for d in EARLY:
        xv(d).start()

    def put(dst, x):
        dst[0], dst[1] = split(x)

    for i in (3, 4, 5):
        loads[i].wait()
    put(ma, va[...])
    put(mb, vb[...])

    landed(buf1, r1)
    low = lax.broadcasted_iota(jnp.int32, (128, 128), 1) < 64
    pre = dot3(both(ma), split(buf1[...]), False)
    re, im = pre[:128], pre[128:]
    yre = re * vwa[0] - im * vwa[1]
    yim = re * vwa[1] + im * vwa[0]
    pre = dot3(both(mb), split(jnp.concatenate([yre, yim], axis=1)), True)
    re, im = pre[:128], pre[128:]
    snd2[pl.ds(0, 128, stride=2)] = jnp.where(low, re, swap(im))
    snd2[pl.ds(1, 128, stride=2)] = jnp.where(low, swap(re), im)

    spread(z_peers, snd2, buf2, mz, mz, 16, s2, r2)

    for i in (6, 7, 8):
        loads[i].wait()
    put(md, vd[...])
    put(me2, ve[...])
    put(mat, va[...].T)
    put(met, ve[...].T)
    put(mdt, jnp.concatenate([vd[:256].T, vd[256:].T], axis=0))
    vwdt[0] = vwd[0, :, :].T
    vwdt[1] = vwd[1, :, :].T

    landed(buf2, r2)
    for i in range(16):
        snd3[16 * i : 16 * i + 16] = buf2[pl.ds(i, 16, stride=16)]

    spread(y_peers, snd3, buf3, my_row, my_u, 16, s3, r3)
    for d in LATE:
        xv(d).start()
    landed(buf3, r3)

    x = jnp.concatenate([buf3[:256], buf3[256:]], axis=1)
    pre = dot3(both(md), split(x), False)
    sign = jnp.where(lax.broadcasted_iota(jnp.int32, (256, 128), 1) < 64, 1.0, -1.0)
    parts = []
    for t in range(2):
        lanes = slice(128 * t, 128 * t + 128)
        y = pre[:256, lanes] + sign * swap(pre[256:, lanes])
        parts.append(y * vwd[0] + swap(y) * vwd[1])
    fs[...] = dot3(both(me2), split(jnp.concatenate(parts, axis=0)), True)

    def point(first, group, m, _):
        lo, hi = pl.ds(pl.multiple_of(8 * m, 8), 8), pl.ds(pl.multiple_of(64 + 8 * m, 8), 8)
        lane = pl.ds(pl.multiple_of(256 * m, 256), 256)
        f0r, f1r = fs[lo, :256], fs[lo, 256:]
        f0i, f1i = fs[hi, :256], fs[hi, 256:]
        if first:
            sums = [jnp.zeros((8, 256), F32)] * 4
        else:
            sums = [ws[lo, :256], ws[hi, :256], ws[lo, 256:], ws[hi, 256:]]
        for d in group:
            who = turn(mx, 4 - d // 2, 4) * 2 + es[d % 2]
            pair = prm[pl.ds(who, 1)][0]
            off, damp = pair[0:1, 0:1], pair[1:2, 0:1]
            if d == 0:
                vr, vi, w = (vsend[pl.ds(mo, 1), p, :, lane][0] for p in range(3))
            else:
                vr, vi, w = (vrecv[d - 1, p, :, lane] for p in range(3))
            dr = vr - w * (f0r + off * f1r)
            di = vi - w * (f0i + off * f1i)
            k = 1.0 / (1.0 + damp * (dr * dr + di * di))
            wr, wi = k * dr, k * di
            sums = [sums[0] + wr, sums[1] + wi, sums[2] + off * wr, sums[3] + off * wi]
        ws[lo, :256], ws[hi, :256], ws[lo, 256:], ws[hi, 256:] = sums
        return 0

    for d in EARLY:
        xp(d).wait_recv()
        xv(d).wait_recv()
    lax.fori_loop(0, 8, functools.partial(point, True, (0,) + EARLY), 0)
    for d in LATE:
        xp(d).wait_recv()
        xv(d).wait_recv()
    lax.fori_loop(0, 8, functools.partial(point, False, LATE), 0)

    pre = dot3(both(met), split(ws[...]), False)
    parts = []
    for t in range(2):
        re, im = pre[:64, 256 * t : 256 * t + 256], pre[64:, 256 * t : 256 * t + 256]
        parts += [re * vwdt[0, :64] - im * vwdt[1, :64], im * vwdt[0, :64] + re * vwdt[1, :64]]
    back = dot3(both(mdt), split(jnp.concatenate(parts, axis=0)), True)
    for t in range(2):
        lanes = slice(128 * t, 128 * t + 128)
        snd5[256 * t : 256 * t + 256] = back[:256, lanes] - sign * swap(back[256:, lanes])

    spread(y_peers, snd5, buf5, mp * 16 + my_u, my_row, 16, s5, r5, 1)
    landed(buf5, r5)
    for i in range(16):
        b = 16 * i
        snd6[pl.ds(i, 16, stride=16)] = buf5[b : b + 16] + buf5[256 + b : 272 + b]

    spread(z_peers, snd6, buf6, mz, mz, 16, s6, r6)
    landed(buf1.at[: 8 * (NC - 1)], s1)
    landed(buf2.at[: 16 * (NZ - 1)], s2)
    landed(buf3.at[: 16 * (NY - 1)], s3)
    landed(buf5.at[: 16 * (NY - 1)], s5)
    landed(prm.at[:7], sp)
    landed(vrecv, sv)
    landed(buf6, r6)
    p0, p1 = buf6[pl.ds(0, 128, stride=2)], buf6[pl.ds(1, 128, stride=2)]
    re, im = jnp.where(low, p0, swap(p1)), jnp.where(low, swap(p0), p1)
    z = dot3(split(jnp.concatenate([re.T, im.T], axis=1)), both(mb), False)
    re, im = z[:, :128], z[:, 128:]
    z = jnp.concatenate([re * vwa[0] + im * vwa[1], im * vwa[0] - re * vwa[1]], axis=0)
    snd7[...] = dot3(both(mat), split(z), False)

    spread(chan_peers, snd7, buf7, chan, chan, 8, s7, r7)
    landed(buf7, r7)
    landed(buf6.at[: 16 * (NZ - 1)], s6)
    landed(buf7.at[: 8 * (NC - 1)], s7)
    out[...] = buf7[...]


def local(taylor_models, gridded_vis, uv_weight, freq_ratio, robust_scale):
    tabs = [jnp.asarray(x) for x in tables()]
    any_space = pl.BlockSpec(memory_space=pltpu.HBM)
    v = pltpu.VMEM
    dma = pltpu.SemaphoreType.DMA
    scratch = (
        [pltpu.SMEM((1,), F32), pltpu.SMEM((1,), F32), v((128, 128), F32), v((2, 64, PIX), BF16), v((64, PIX), BF16)]
        + [v(x.shape, F32) for x in tabs]
        + [v((2, *s), BF16) for s in
           ((256, 128), (128, 256), (256, 256), (512, 256), (512, 256), (128, 128), (128, 128))]
        + [v((2, 128, 256), F32)]
        + [v((n, m), F32) for n, m in
           ((128, 128), (256, 128), (256, 128), (256, 128), (512, 128), (128, 512), (128, 512),
            (512, 128), (512, 128), (256, 128), (256, 128), (128, 128), (128, 128))]
        + [v((8, 3, 8, PIX), F32), v((7, 3, 8, PIX), F32), v((8, 8, 128), F32)]
        + [dma((11,))] + [dma] * 8 + [dma] * 6 + [dma((8,)), dma((8,))]
    )
    out = pl.pallas_call(
        kernel,
        out_shape=jax.ShapeDtypeStruct((128, 128), F32),
        in_specs=[any_space] * 11,
        out_specs=pl.BlockSpec(memory_space=pltpu.VMEM),
        scratch_shapes=scratch,
        compiler_params=pltpu.CompilerParams(
            collective_id=0, has_side_effects=True, vmem_limit_bytes=66_000_000),
    )(freq_ratio, robust_scale, taylor_models.reshape(128, 128), gridded_vis[0], uv_weight[0], *tabs)
    return out.reshape(2, 64, 128)


def solution(mesh):
    placed = (
        P(None, "slab", "chan"),
        P("chan", None, "slab", None),
        P("chan", "slab", None),
        P("chan"),
        P("chan"),
    )
    return jax.shard_map(
        local, mesh=mesh, in_specs=placed, out_specs=P(None, "slab", "chan"), check_vma=False
    )
```

time: 86.9 us -> 66.9 us (0.77)
  Pallas kernels: 75.8 us -> 63.9 us
  local copies, waits for them, and re-layouts: 9.34 us -> 1.47 us
    pallas_call x1, Pallas kernels: 75.8 us -> 63.9 us  [local(): pl.pallas_call(kernel, out_shape=jax.ShapeDtypeStruct((128, 128), F32), i...]
    unnamed x19 -> x1, local copies, waits for them, and re-layouts: 9.34 us -> 1.47 us
where the time goes in v1:
time: 66.9 us; the launch traced here: 66.7 us
  Pallas kernels  63.9 us (96%)
  local copies, waits for them, and re-layouts  1.47 us (2%)
  between operations  1.3 us (2%)
    pallas_call x1, Pallas kernels, local(): pl.pallas_call(kernel, out_shape=jax.ShapeDtypeStruct((128, 128), F32), i...  63.9 us
    unnamed x1, local copies, waits for them, and re-layouts  1.47 us

profile of v1, /device:TPU:1, one launch (start us, length us, event | category | flops | bytes accessed | tf_op | source)
XLA Modules:
  0.0 66.7 jit_solution(16486981455074943806)
XLA Ops:
  1.3 63.9 %shard_map.109 = f32[128,128]{1,0:T(8,128)} custom-call(f32[1]{0:T(128)S(6)} %copy.13.freq, f32[1]{0:T(128)S(6)} %copy.14.robust, f32[128,128]{1,0:T(8,128)} %bitcast.7, bf16[2,64,2048]{2,1,0:T(8,128)(2,1)} %bitcast.4, bf16[64,2048]{1,0:T(8,128)(2,1)} %bitcast.6, f32[256,128]{1,0:T(8,128)} %constant.12.clone.t_a, f32[2,128,128]{2,1,0:T(8,128)} %constant.13.clone.w_a, ...), custom_call_target="tpu_custom_call" | custom-call | tf_op jit(solution)/shard_map/pallas_call | solution.py:309
  65.2 1.5 %copy.15 = f32[2,64,128]{2,1,0:T(8,128)} copy(f32[2,64,128]{2,1,0:T(8,128)} %bitcast.5) | data formatting | bytes 131072

commit v2 on v1

--- a/solution.py
+++ b/solution.py
@@ -14,7 +14,7 @@
 NC, NZ, NY = 16, 16, 32
 
 
-EARLY, LATE = (2, 6, 1, 3, 7), (4, 5)
+EARLY, LATE, CUT = (1, 5, 4, 2, 6, 3), (7,), 1
 
 
 def rep(angle):
@@ -84,18 +84,21 @@
     mz = z * 2 + mk
     mo = mx * 2 + me
     xs, ys = [turn(mx, d, 4) for d in range(4)], [turn(my, d, 4) for d in range(4)]
-    hs, ks = [mh, 1 - mh], [mk, 1 - mk]
-    es = [lax.rem(y, 2) for y in ys]
+    ks, es = [mk, 1 - mk], [me, 1 - me]
+    ring = [turn(mh * 4 + my, d, 8) for d in range(8)]
     x_rows = [lax.div(x, 2) * 16 + lax.rem(x, 2) * 4 for x in xs]
-    slab_h = [slab, slab + 2 - 4 * mh]
     FAR = (2, 3, 1, 0)
 
     chan_peers = [
         (xs[i] * 4 + ys[j], {"chan": xs[i] * 4 + ys[j]}) for i in FAR for j in FAR if i or j]
-    y_peers = [
-        (hs[h] * 8 + xs[i] * 2 + es[j], x_rows[i] + hs[h] * 8 + ys[j],
-         {"chan": xs[i] * 4 + ys[j], "slab": slab_h[h]})
-        for h in (1, 0) for i in FAR for j in FAR if h or i or j]
+    y_peers = []
+    for j in (4, 3, 5, 2, 6, 1, 7, 0):
+        half, y = lax.div(ring[j], 4), lax.rem(ring[j], 4)
+        side, there = half * 8 + lax.rem(y, 2), slab + 2 * (half - mh)
+        for i in FAR:
+            if i or j:
+                y_peers.append((side + xs[i] * 2, x_rows[i] + half * 8 + y,
+                                {"chan": xs[i] * 4 + y, "slab": there}))
     z_peers = []
     for d in (4, 3, 5, 2, 6, 1, 7, 0):
         for k in (1, 0):
@@ -157,15 +160,23 @@
         return pltpu.make_async_remote_copy(
             prm.at[mo], prm.at[mo], sp, rp.at[d], device_id=ally(d)[1], device_id_type=MESH)
 
-    def xv(d):
+    def xv(d, planes):
         o, device = ally(d)
-        return pltpu.make_async_remote_copy(
-            vsend.at[o], vrecv.at[d - 1], sv, rv.at[d], device_id=device, device_id_type=MESH)
+        for p in planes:
+            pltpu.make_async_remote_copy(
+                vsend.at[o, p], vrecv.at[d - 1, p], sv, rv.at[d],
+                device_id=device, device_id_type=MESH).start()
+
+    def arrived(d):
+        xp(d).wait_recv()
+        landed(vrecv.at[d - 1], rv.at[d])
 
     for d in EARLY + LATE:
         xp(d).start()
     for d in EARLY:
-        xv(d).start()
+        xv(d, range(3))
+    for d in LATE:
+        xv(d, range(CUT))
 
     def put(dst, x):
         dst[0], dst[1] = split(x)
@@ -204,7 +215,7 @@
 
     spread(y_peers, snd3, buf3, my_row, my_u, 16, s3, r3)
     for d in LATE:
-        xv(d).start()
+        xv(d, range(CUT, 3))
     landed(buf3, r3)
 
     x = jnp.concatenate([buf3[:256], buf3[256:]], axis=1)
@@ -243,12 +254,10 @@
         return 0
 
     for d in EARLY:
-        xp(d).wait_recv()
-        xv(d).wait_recv()
+        arrived(d)
     lax.fori_loop(0, 8, functools.partial(point, True, (0,) + EARLY), 0)
     for d in LATE:
-        xp(d).wait_recv()
-        xv(d).wait_recv()
+        arrived(d)
     lax.fori_loop(0, 8, functools.partial(point, False, LATE), 0)
 
     pre = dot3(both(met), split(ws[...]), False)
@@ -308,7 +317,7 @@
     )
     out = pl.pallas_call(
         kernel,
-        out_shape=jax.ShapeDtypeStruct((128, 128), F32),
+        out_shape=pltpu.VMEM((128, 128), F32),
         in_specs=[any_space] * 11,
         out_specs=pl.BlockSpec(memory_space=pltpu.VMEM),
         scratch_shapes=scratch,

time: 66.9 us -> 64 us (0.957)
  Pallas kernels: 63.9 us -> 61.9 us
  local copies, waits for them, and re-layouts: 1.47 us -> 0.63 us
    pallas_call x1, Pallas kernels: 63.9 us -> 61.9 us  [local(): pl.pallas_call(kernel, out_shape=pltpu.VMEM((128, 128), F32), in_specs=[a...]
    unnamed x1, local copies, waits for them, and re-layouts: 1.47 us -> 0.63 us
where the time goes in v2:
time: 64 us; the launch traced here: 63.9 us
  Pallas kernels  61.9 us (97%)
  between operations  1.3 us (2%)
    pallas_call x1, Pallas kernels, local(): pl.pallas_call(kernel, out_shape=pltpu.VMEM((128, 128), F32), in_specs=[a...  61.9 us

profile of v2, /device:TPU:1, one launch (start us, length us, event | category | flops | bytes accessed | tf_op | source)
XLA Modules:
  0.0 63.9 jit_solution(4187254597426003812)
XLA Ops:
  1.3 61.9 %shard_map.109 = f32[128,128]{1,0:T(8,128)S(1)} custom-call(f32[1]{0:T(128)S(6)} %copy.14.freq, f32[1]{0:T(128)S(6)} %copy.15.robust, f32[128,128]{1,0:T(8,128)} %bitcast.7, bf16[2,64,2048]{2,1,0:T(8,128)(2,1)} %bitcast.5, bf16[64,2048]{1,0:T(8,128)(2,1)} %bitcast.6, f32[256,128]{1,0:T(8,128)} %constant.12.clone.t_a, f32[2,128,128]{2,1,0:T(8,128)} %constant.13.clone.w_a, ...), custom_call_target="tpu_custom_call" | custom-call | tf_op jit(solution)/shard_map/pallas_call | solution.py:318
  63.2 0.6 copy.13

commit v3 on v2

--- a/solution.py
+++ b/solution.py
@@ -14,7 +14,9 @@
 NC, NZ, NY = 16, 16, 32
 
 
-EARLY, LATE, CUT = (1, 5, 4, 2, 6, 3), (7,), 1
+THIRD = ((7, 1), (7, 2))
+SECOND = tuple((d, p) for d in (1, 5, 4, 2, 6, 3, 7) for p in range(3) if (d, p) not in THIRD)
+EARLY, LATE = (1, 5, 4, 2, 6, 3), (7,)
 
 
 def rep(angle):
@@ -72,7 +74,7 @@
     ma, mat, mb, md, mdt, me2, met, vwdt,
     buf1, snd2, buf2, snd3, buf3, fs, ws, snd5, buf5, snd6, buf6, snd7, buf7,
     vsend, vrecv, prm,
-    lsem, s1, s2, s3, s5, s6, s7, sv, sp, r1, r2, r3, r5, r6, r7, rv, rp,
+    lsem, s1, s2, s3, s5, s6, s7, sv, sp, r1, r2, r3, r5, r6, r7, rv, rp, hello,
 ):
     def turn(i, d, n):
         return lax.rem(i + d, n)
@@ -108,8 +110,17 @@
     my_row, my_u = x_rows[0] + mh * 8 + my, mh * 8 + mo
 
     barrier = pltpu.get_barrier_semaphore()
-    for peer in y_peers + z_peers:
-        pl.semaphore_signal(barrier, inc=1, device_id=peer[-1], device_id_type=MESH)
+    allies = [{"chan": xs[i] * 4 + mp * 2 + es[e]} for i in (2, 3, 1) for e in (1, 0)]
+    ring_near = [{"chan": mx * 4 + lax.rem(ring[j], 4), "slab": slab + 2 * (lax.div(ring[j], 4) - mh)}
+                 for j in (3, 5, 2, 6, 1, 7)]
+
+    def z_at(d, k):
+        return {"slab": turn(z, d, 8) * 4 + mh * 2 + ks[k]}
+
+    z_near = [z_at(3, 0), z_at(5, 0), z_at(2, 0), z_at(6, 0), z_at(1, 1), z_at(7, 1), z_at(1, 0), z_at(7, 0), z_at(0, 1)]
+    near = [peer[-1] for peer in chan_peers] + ring_near + z_near
+    for device in near:
+        pl.semaphore_signal(barrier, inc=1, device_id=device, device_id_type=MESH)
 
     loads = [
         pltpu.make_async_copy(src, dst, lsem.at[i])
@@ -135,7 +146,11 @@
             vsend[2 * q + 1, p] = wide[8:]
     loads[0].wait()
 
-    pl.semaphore_wait(barrier, len(y_peers) + len(z_peers))
+    pl.semaphore_wait(barrier, len(near))
+
+    told = allies + [{"chan": mx * 4 + mp * 2 + es[1]}, z_at(0, 1), z_at(7, 0), z_at(7, 1)]
+    for device in told:
+        pl.semaphore_signal(hello, inc=1, device_id=device, device_id_type=MESH)
 
     def tile(ref, i, n=8):
         return ref.at[pl.ds(pl.multiple_of(i * n, n), n)]
@@ -150,8 +165,6 @@
     def landed(buf, sem):
         pltpu.make_async_copy(buf, buf, sem).wait()
 
-    spread(chan_peers, tay_v, buf1, chan, chan, 8, s1, r1)
-
     def ally(d):
         x, e = xs[d // 2], es[d % 2]
         return x * 2 + e, {"chan": x * 4 + mp * 2 + e}
@@ -160,9 +173,9 @@
         return pltpu.make_async_remote_copy(
             prm.at[mo], prm.at[mo], sp, rp.at[d], device_id=ally(d)[1], device_id_type=MESH)
 
-    def xv(d, planes):
-        o, device = ally(d)
-        for p in planes:
+    def xv(which):
+        for d, p in which:
+            o, device = ally(d)
             pltpu.make_async_remote_copy(
                 vsend.at[o, p], vrecv.at[d - 1, p], sv, rv.at[d],
                 device_id=device, device_id_type=MESH).start()
@@ -171,12 +184,11 @@
         xp(d).wait_recv()
         landed(vrecv.at[d - 1], rv.at[d])
 
+    spread(chan_peers, tay_v, buf1, chan, chan, 8, s1, r1)
+
     for d in EARLY + LATE:
         xp(d).start()
-    for d in EARLY:
-        xv(d, range(3))
-    for d in LATE:
-        xv(d, range(CUT))
+    xv(SECOND)
 
     def put(dst, x):
         dst[0], dst[1] = split(x)
@@ -197,6 +209,8 @@
     snd2[pl.ds(0, 128, stride=2)] = jnp.where(low, re, swap(im))
     snd2[pl.ds(1, 128, stride=2)] = jnp.where(low, swap(re), im)
 
+    pl.semaphore_wait(hello, len(told))
+
     spread(z_peers, snd2, buf2, mz, mz, 16, s2, r2)
 
     for i in (6, 7, 8):
@@ -214,8 +228,7 @@
         snd3[16 * i : 16 * i + 16] = buf2[pl.ds(i, 16, stride=16)]
 
     spread(y_peers, snd3, buf3, my_row, my_u, 16, s3, r3)
-    for d in LATE:
-        xv(d, range(CUT, 3))
+    xv(THIRD)
     landed(buf3, r3)
 
     x = jnp.concatenate([buf3[:256], buf3[256:]], axis=1)
@@ -255,10 +268,10 @@
 
     for d in EARLY:
         arrived(d)
-    lax.fori_loop(0, 8, functools.partial(point, True, (0,) + EARLY), 0)
+    lax.fori_loop(0, 8, functools.partial(point, True, (0,) + EARLY), 0, unroll=True)
     for d in LATE:
         arrived(d)
-    lax.fori_loop(0, 8, functools.partial(point, False, LATE), 0)
+    lax.fori_loop(0, 8, functools.partial(point, False, LATE), 0, unroll=True)
 
     pre = dot3(both(met), split(ws[...]), False)
     parts = []
@@ -313,7 +326,7 @@
            ((128, 128), (256, 128), (256, 128), (256, 128), (512, 128), (128, 512), (128, 512),
             (512, 128), (512, 128), (256, 128), (256, 128), (128, 128), (128, 128))]
         + [v((8, 3, 8, PIX), F32), v((7, 3, 8, PIX), F32), v((8, 8, 128), F32)]
-        + [dma((11,))] + [dma] * 8 + [dma] * 6 + [dma((8,)), dma((8,))]
+        + [dma((11,))] + [dma] * 8 + [dma] * 6 + [dma((8,)), dma((8,))] + [pltpu.SemaphoreType.REGULAR]
     )
     out = pl.pallas_call(
         kernel,

time: 64 us -> 62.3 us (0.973)
  Pallas kernels: 61.9 us -> 60.3 us
    pallas_call x1, Pallas kernels: 61.9 us -> 60.3 us  [local(): pl.pallas_call(kernel, out_shape=pltpu.VMEM((128, 128), F32), in_specs=[a...]
where the time goes in v3:
time: 62.3 us; the launch traced here: 62.2 us
  Pallas kernels  60.3 us (97%)
  between operations  1.3 us (2%)
  local copies, waits for them, and re-layouts  0.63 us (1%)
    pallas_call x1, Pallas kernels, local(): pl.pallas_call(kernel, out_shape=pltpu.VMEM((128, 128), F32), in_specs=[a...  60.3 us

profile of v3, /device:TPU:1, one launch (start us, length us, event | category | flops | bytes accessed | tf_op | source)
XLA Modules:
  0.0 62.2 jit_solution(8013807022460568053)
XLA Ops:
  1.3 60.3 %shard_map.109 = f32[128,128]{1,0:T(8,128)S(1)} custom-call(f32[1]{0:T(128)S(6)} %copy.14.freq, f32[1]{0:T(128)S(6)} %copy.15.robust, f32[128,128]{1,0:T(8,128)} %bitcast.7, bf16[2,64,2048]{2,1,0:T(8,128)(2,1)} %bitcast.5, bf16[64,2048]{1,0:T(8,128)(2,1)} %bitcast.6, f32[256,128]{1,0:T(8,128)} %constant.12.clone.t_a, f32[2,128,128]{2,1,0:T(8,128)} %constant.13.clone.w_a, ...), custom_call_target="tpu_custom_call" | custom-call | tf_op jit(solution)/shard_map/pallas_call | solution.py:331
  61.6 0.6 %copy.13 = f32[2,64,128]{2,1,0:T(8,128)} copy(f32[2,64,128]{2,1,0:T(8,128)S(1)} %bitcast.4) | data formatting | bytes 131072

commit v4 on v3

--- a/solution.py
+++ b/solution.py
@@ -219,7 +219,10 @@
     put(me2, ve[...])
     put(mat, va[...].T)
     put(met, ve[...].T)
-    put(mdt, jnp.concatenate([vd[:256].T, vd[256:].T], axis=0))
+    turned = (vd[:256].T, vd[256:].T)
+    for a in range(2):
+        put(mdt.at[a], jnp.concatenate(
+            [x[16 * i + 8 * a : 16 * i + 8 * a + 8] for x in turned for i in range(16)], axis=0))
     vwdt[0] = vwd[0, :, :].T
     vwdt[1] = vwd[1, :, :].T
 
@@ -278,22 +281,39 @@
     for t in range(2):
         re, im = pre[:64, 256 * t : 256 * t + 256], pre[64:, 256 * t : 256 * t + 256]
         parts += [re * vwdt[0, :64] - im * vwdt[1, :64], im * vwdt[0, :64] + re * vwdt[1, :64]]
-    back = dot3(both(mdt), split(jnp.concatenate(parts, axis=0)), True)
-    for t in range(2):
-        lanes = slice(128 * t, 128 * t + 128)
-        snd5[256 * t : 256 * t + 256] = back[:256, lanes] - sign * swap(back[256:, lanes])
-
-    spread(y_peers, snd5, buf5, mp * 16 + my_u, my_row, 16, s5, r5, 1)
-    landed(buf5, r5)
-    for i in range(16):
-        b = 16 * i
-        snd6[pl.ds(i, 16, stride=16)] = buf5[b : b + 16] + buf5[256 + b : 272 + b]
-
-    spread(z_peers, snd6, buf6, mz, mz, 16, s6, r6)
+    y = split(jnp.concatenate(parts, axis=0))
+    far_half = 1 - lax.div(z, 4)
+    halves = (far_half, 1 - far_half)
+    sign = sign[:128]
+
+    mine = mp * 16 + my_u
+    for o, a in enumerate(halves):
+        back = dot3((mdt[a, 0], mdt[a, 1]), y, True)
+        for t in range(2):
+            lanes = slice(128 * t, 128 * t + 128)
+            snd5[o, 128 * t : 128 * t + 128] = back[:128, lanes] - sign * swap(back[128:, lanes])
+        spread(y_peers, snd5.at[o], buf5.at[o], mine, my_row, 8, s5.at[o], r5.at[o], 1)
+
+    for o, a in enumerate(halves):
+        landed(buf5.at[o], r5.at[o])
+        for i in range(16):
+            b = 8 * i
+            snd6[o, pl.ds(i, 8, stride=16)] = buf5[o, b : b + 8] + buf5[o, 128 + b : 136 + b]
+        own = lax.rem(mz, 8)
+        for d in (4, 3, 5, 2, 6, 1, 7, 0):
+            n = turn(own, d, 8)
+            if d or o == 0:
+                pltpu.make_async_remote_copy(
+                    tile(snd6.at[o], n, 16), tile(buf6, mz, 16), s6, r6,
+                    device_id={"slab": (a * 4 + lax.div(n, 2)) * 4 + mh * 2 + lax.rem(n, 2)},
+                    device_id_type=MESH).start()
+            else:
+                pltpu.make_async_copy(tile(snd6.at[o], n, 16), tile(buf6, mz, 16), r6).start()
     landed(buf1.at[: 8 * (NC - 1)], s1)
     landed(buf2.at[: 16 * (NZ - 1)], s2)
     landed(buf3.at[: 16 * (NY - 1)], s3)
-    landed(buf5.at[: 16 * (NY - 1)], s5)
+    for o in range(2):
+        landed(buf5.at[o, : 8 * (NY - 1)], s5.at[o])
     landed(prm.at[:7], sp)
     landed(vrecv, sv)
     landed(buf6, r6)
@@ -320,13 +340,13 @@
         [pltpu.SMEM((1,), F32), pltpu.SMEM((1,), F32), v((128, 128), F32), v((2, 64, PIX), BF16), v((64, PIX), BF16)]
         + [v(x.shape, F32) for x in tabs]
         + [v((2, *s), BF16) for s in
-           ((256, 128), (128, 256), (256, 256), (512, 256), (512, 256), (128, 128), (128, 128))]
+           ((256, 128), (128, 256), (256, 256), (512, 256), (2, 256, 256), (128, 128), (128, 128))]
         + [v((2, 128, 256), F32)]
-        + [v((n, m), F32) for n, m in
+        + [v(s, F32) for s in
            ((128, 128), (256, 128), (256, 128), (256, 128), (512, 128), (128, 512), (128, 512),
-            (512, 128), (512, 128), (256, 128), (256, 128), (128, 128), (128, 128))]
+            (2, 256, 128), (2, 256, 128), (2, 128, 128), (256, 128), (128, 128), (128, 128))]
         + [v((8, 3, 8, PIX), F32), v((7, 3, 8, PIX), F32), v((8, 8, 128), F32)]
-        + [dma((11,))] + [dma] * 8 + [dma] * 6 + [dma((8,)), dma((8,))] + [pltpu.SemaphoreType.REGULAR]
+        + [dma((11,)), dma, dma, dma, dma((2,)), dma, dma, dma, dma, dma, dma, dma, dma((2,)), dma, dma, dma((8,)), dma((8,))] + [pltpu.SemaphoreType.REGULAR]
     )
     out = pl.pallas_call(
         kernel,

time: 62.3 us -> 62.1 us (level)
  no operation moved by 1% of the time
where the time goes in v4:
time: 62.1 us; the launch traced here: 61.9 us
  Pallas kernels  60 us (97%)
  between operations  1.3 us (2%)
  local copies, waits for them, and re-layouts  0.63 us (1%)
    pallas_call x1, Pallas kernels, local(): pl.pallas_call(kernel, out_shape=pltpu.VMEM((128, 128), F32), in_specs=[a...  60 us

profile of v4, /device:TPU:1, one launch (start us, length us, event | category | flops | bytes accessed | tf_op | source)
XLA Modules:
  0.0 61.9 jit_solution(13146791782742502639)
XLA Ops:
  1.3 60.0 %shard_map.109 = f32[128,128]{1,0:T(8,128)S(1)} custom-call(f32[1]{0:T(128)S(6)} %copy.14.freq, f32[1]{0:T(128)S(6)} %copy.15.robust, f32[128,128]{1,0:T(8,128)} %bitcast.7, bf16[2,64,2048]{2,1,0:T(8,128)(2,1)} %bitcast.5, bf16[64,2048]{1,0:T(8,128)(2,1)} %bitcast.6, f32[256,128]{1,0:T(8,128)} %constant.12.clone.t_a, f32[2,128,128]{2,1,0:T(8,128)} %constant.13.clone.w_a, ...), custom_call_target="tpu_custom_call" | custom-call | tf_op jit(solution)/shard_map/pallas_call | solution.py:351
  61.3 0.6 %copy.13 = f32[2,64,128]{2,1,0:T(8,128)} copy(f32[2,64,128]{2,1,0:T(8,128)S(1)} %bitcast.4) | data formatting | bytes 131072

commit v5 on v4

--- a/solution.py
+++ b/solution.py
@@ -14,7 +14,7 @@
 NC, NZ, NY = 16, 16, 32
 
 
-THIRD = ((7, 1), (7, 2))
+THIRD = ((7, 2),)
 SECOND = tuple((d, p) for d in (1, 5, 4, 2, 6, 3, 7) for p in range(3) if (d, p) not in THIRD)
 EARLY, LATE = (1, 5, 4, 2, 6, 3), (7,)
 
@@ -27,11 +27,12 @@
 def tables():
     tau = 2 * np.pi
     j, c = np.arange(16), np.arange(16)
-    ang = tau * np.outer(j, c) / 16
+    ang = (tau * np.outer(j, c) / 16).reshape(2, 8, 16)
     first = np.stack([np.cos(ang), -np.sin(ang)])
-    t_a = np.einsum("ijc,rq->ijrcq", first, np.eye(8)).reshape(256, 128)
+    t_a = np.einsum("iejc,rq->ierjcq", first, np.eye(8)).reshape(256, 128)
     ang = np.repeat(tau * np.outer(j, np.arange(128)) / PIX, 8, axis=0)
     w_a = np.stack([np.cos(ang), -np.sin(ang)])
+    w_b = w_a.reshape(2, 2, 8, 8, 128).swapaxes(2, 3).reshape(2, 128, 128)
     z, k, h, q = np.meshgrid(*map(np.arange, (8, 2, 2, 4)), indexing="ij")
     step = (((z * 2 + h) * 2 + k) * 4 + q).reshape(128)
     t_b = np.einsum("oika->okia", rep(tau * np.outer(step, np.arange(128)) / 128)).reshape(256, 256)
@@ -43,7 +44,36 @@
     w_d = np.stack([np.tile(np.cos(ang), (1, 2)), np.concatenate([np.sin(ang), -np.sin(ang)], axis=1)]) / PIX
     e = rep(tau * np.outer(np.arange(8), np.arange(8)) / 8)
     t_e = np.einsum("oimr,jq->omjiqr", e, np.eye(8)).reshape(128, 128)
-    return [x.astype(np.float32) for x in (t_a, w_a, t_b, t_d, w_d, t_e)]
+    return [x.astype(np.float32) for x in (t_a, w_a, t_b, t_d, w_d, t_e, w_b)]
+
+
+def combine(a, b, sign):
+    if b is None:
+        return a
+    if a is None:
+        return b if sign > 0 else -b
+    return a + b if sign > 0 else a - b
+
+
+def twist(x, k, n, sign):
+    re, im = x
+    if k == 0:
+        return x
+    if 4 * k == n:
+        return (None if im is None else -sign * im, sign * re)
+    c, s = float(np.cos(2 * np.pi * k / n)), float(sign * np.sin(2 * np.pi * k / n))
+    if im is None:
+        return c * re, s * re
+    return c * re - s * im, c * im + s * re
+
+
+def transform(xs, sign):
+    n = len(xs)
+    if n == 1:
+        return xs
+    even, odd = transform(xs[::2], sign), transform(xs[1::2], sign)
+    odd = [twist(x, k, n, sign) for k, x in enumerate(odd)]
+    return [tuple(combine(p, q, side) for p, q in zip(a, b)) for side in (1, -1) for a, b in zip(even, odd)]
 
 
 def split(x):
@@ -69,9 +99,9 @@
 
 
 def kernel(
-    freq, robust, taylor, vis, wt, t_a, w_a, t_b, t_d, w_d, t_e, out,
-    freq_s, robust_s, tay_v, vis_v, wt_v, va, vwa, vb, vd, vwd, ve,
-    ma, mat, mb, md, mdt, me2, met, vwdt,
+    freq, robust, taylor, vis, wt, t_a, w_a, t_b, t_d, w_d, t_e, w_b, out,
+    freq_s, robust_s, tay_v, vis_v, wt_v, va, vwa, vb, vd, vwd, ve, vwb,
+    mat, mb, md, mdt, me2, vwdt,
     buf1, snd2, buf2, snd3, buf3, fs, ws, snd5, buf5, snd6, buf6, snd7, buf7,
     vsend, vrecv, prm,
     lsem, s1, s2, s3, s5, s6, s7, sv, sp, r1, r2, r3, r5, r6, r7, rv, rp, hello,
@@ -126,10 +156,10 @@
         pltpu.make_async_copy(src, dst, lsem.at[i])
         for i, (src, dst) in enumerate(
             [(taylor, tay_v), (vis, vis_v), (wt, wt_v), (t_a, va), (w_a, vwa),
-             (t_b, vb), (t_d, vd), (w_d, vwd), (t_e, ve), (freq, freq_s), (robust, robust_s)]
+             (t_b, vb), (t_d, vd), (w_d, vwd), (t_e, ve), (freq, freq_s), (robust, robust_s), (w_b, vwb)]
         )
     ]
-    for i in (9, 10, 0, 1, 2, 3, 4, 5, 6, 7, 8):
+    for i in (9, 10, 0, 1, 2, 4, 5, 6, 7, 8, 3, 11):
         loads[i].start()
 
     rows = lax.broadcasted_iota(jnp.int32, (8, 128), 0)
@@ -193,15 +223,16 @@
     def put(dst, x):
         dst[0], dst[1] = split(x)
 
-    for i in (3, 4, 5):
+    for i in (4, 5):
         loads[i].wait()
-    put(ma, va[...])
     put(mb, vb[...])
 
     landed(buf1, r1)
     low = lax.broadcasted_iota(jnp.int32, (128, 128), 1) < 64
-    pre = dot3(both(ma), split(buf1[...]), False)
-    re, im = pre[:128], pre[128:]
+    rows_in = [(buf1[8 * i : 8 * i + 8], None) for i in range(16)]
+    rows_out = transform(rows_in, -1.0)
+    re = jnp.concatenate([x[0] for x in rows_out], axis=0)
+    im = jnp.concatenate([jnp.zeros((8, 128), F32) if x[1] is None else x[1] for x in rows_out], axis=0)
     yre = re * vwa[0] - im * vwa[1]
     yim = re * vwa[1] + im * vwa[0]
     pre = dot3(both(mb), split(jnp.concatenate([yre, yim], axis=1)), True)
@@ -213,12 +244,11 @@
 
     spread(z_peers, snd2, buf2, mz, mz, 16, s2, r2)
 
-    for i in (6, 7, 8):
+    for i in (6, 7, 8, 3, 11):
         loads[i].wait()
     put(md, vd[...])
     put(me2, ve[...])
     put(mat, va[...].T)
-    put(met, ve[...].T)
     turned = (vd[:256].T, vd[256:].T)
     for a in range(2):
         put(mdt.at[a], jnp.concatenate(
@@ -276,11 +306,13 @@
         arrived(d)
     lax.fori_loop(0, 8, functools.partial(point, False, LATE), 0, unroll=True)
 
-    pre = dot3(both(met), split(ws[...]), False)
     parts = []
     for t in range(2):
-        re, im = pre[:64, 256 * t : 256 * t + 256], pre[64:, 256 * t : 256 * t + 256]
-        parts += [re * vwdt[0, :64] - im * vwdt[1, :64], im * vwdt[0, :64] + re * vwdt[1, :64]]
+        lanes = slice(256 * t, 256 * t + 256)
+        around = transform([(ws[8 * m : 8 * m + 8, lanes], ws[64 + 8 * m : 72 + 8 * m, lanes]) for m in range(8)], 1.0)
+        turns = [(vwdt[0, r : r + 1], vwdt[1, r : r + 1]) for r in range(8)]
+        parts += [re * c - im * s for (re, im), (c, s) in zip(around, turns)]
+        parts += [im * c + re * s for (re, im), (c, s) in zip(around, turns)]
     y = split(jnp.concatenate(parts, axis=0))
     far_half = 1 - lax.div(z, 4)
     halves = (far_half, 1 - far_half)
@@ -321,7 +353,7 @@
     re, im = jnp.where(low, p0, swap(p1)), jnp.where(low, swap(p0), p1)
     z = dot3(split(jnp.concatenate([re.T, im.T], axis=1)), both(mb), False)
     re, im = z[:, :128], z[:, 128:]
-    z = jnp.concatenate([re * vwa[0] + im * vwa[1], im * vwa[0] - re * vwa[1]], axis=0)
+    z = jnp.concatenate([re * vwb[0] + im * vwb[1], im * vwb[0] - re * vwb[1]], axis=0)
     snd7[...] = dot3(both(mat), split(z), False)
 
     spread(chan_peers, snd7, buf7, chan, chan, 8, s7, r7)
@@ -340,18 +372,18 @@
         [pltpu.SMEM((1,), F32), pltpu.SMEM((1,), F32), v((128, 128), F32), v((2, 64, PIX), BF16), v((64, PIX), BF16)]
         + [v(x.shape, F32) for x in tabs]
         + [v((2, *s), BF16) for s in
-           ((256, 128), (128, 256), (256, 256), (512, 256), (2, 256, 256), (128, 128), (128, 128))]
+           ((128, 256), (256, 256), (512, 256), (2, 256, 256), (128, 128))]
         + [v((2, 128, 256), F32)]
         + [v(s, F32) for s in
            ((128, 128), (256, 128), (256, 128), (256, 128), (512, 128), (128, 512), (128, 512),
             (2, 256, 128), (2, 256, 128), (2, 128, 128), (256, 128), (128, 128), (128, 128))]
         + [v((8, 3, 8, PIX), F32), v((7, 3, 8, PIX), F32), v((8, 8, 128), F32)]
-        + [dma((11,)), dma, dma, dma, dma((2,)), dma, dma, dma, dma, dma, dma, dma, dma((2,)), dma, dma, dma((8,)), dma((8,))] + [pltpu.SemaphoreType.REGULAR]
+        + [dma((12,)), dma, dma, dma, dma((2,)), dma, dma, dma, dma, dma, dma, dma, dma((2,)), dma, dma, dma((8,)), dma((8,))] + [pltpu.SemaphoreType.REGULAR]
     )
     out = pl.pallas_call(
         kernel,
         out_shape=pltpu.VMEM((128, 128), F32),
-        in_specs=[any_space] * 11,
+        in_specs=[any_space] * 12,
         out_specs=pl.BlockSpec(memory_space=pltpu.VMEM),
         scratch_shapes=scratch,
         compiler_params=pltpu.CompilerParams(

time: 62.1 us -> 61.7 us (level)
  no operation moved by 1% of the time
where the time goes in v5:
time: 61.7 us; the launch traced here: 61.6 us
  Pallas kernels  59.6 us (97%)
  between operations  1.3 us (2%)
  local copies, waits for them, and re-layouts  0.63 us (1%)
    pallas_call x1, Pallas kernels, local(): pl.pallas_call(kernel, out_shape=pltpu.VMEM((128, 128), F32), in_specs=[a...  59.6 us

profile of v5, /device:TPU:1, one launch (start us, length us, event | category | flops | bytes accessed | tf_op | source)
XLA Modules:
  0.0 61.6 jit_solution(6261134673913975328)
XLA Ops:
  1.3 59.6 %shard_map.118 = f32[128,128]{1,0:T(8,128)S(1)} custom-call(f32[1]{0:T(128)S(6)} %copy.15.freq, f32[1]{0:T(128)S(6)} %copy.16.robust, f32[128,128]{1,0:T(8,128)} %bitcast.7, bf16[2,64,2048]{2,1,0:T(8,128)(2,1)} %bitcast.5, bf16[64,2048]{1,0:T(8,128)(2,1)} %bitcast.6, f32[256,128]{1,0:T(8,128)} %constant.14.clone.t_a, f32[2,128,128]{2,1,0:T(8,128)} %constant.15.clone.w_a, ...), custom_call_target="tpu_custom_call" | custom-call | tf_op jit(solution)/shard_map/pallas_call | solution.py:383
  60.9 0.6 %copy.14 = f32[2,64,128]{2,1,0:T(8,128)} copy(f32[2,64,128]{2,1,0:T(8,128)S(1)} %bitcast.4) | data formatting | bytes 131072
